TPU v7x, 256 devices: a whole 4x4x8 slice. The times are simulated.
256 devices in a mesh: nest: 4 (over y), tile: 64 (over z, x, core).
Axes of the slice: x: 4, y: 4, z: 8, core: 2. Of those that a mesh axis runs over, the one named last changes fastest.
Arguments:
- child_fields: float32 [4, 32, 1536, 3072], P('nest', None, 'tile'), may hold values from -18 to 18
- row_weights: float32 [8, 24], replicated
- col_weights: float32 [3072, 1024], replicated
- nest_offsets: int32 [4, 2], replicated, may hold values from 0 to 1023, as said below
- priority: int32 [1024, 1024], P('tile', 'nest'), may hold values from -1 to 3, as said below
- parent_old: float32 [32, 1024, 1024], P(None, 'tile', 'nest'), may hold values from -6 to 6
- smooth_rate: float32 [32], replicated, may hold values from 0.03 to 0.22
Outputs:
- parent_new: float32 [32, 1024, 1024], P(None, 'tile', 'nest')
Inputs may be any that keep to these rules, and one draw needn't show every extreme that they name: nest_offsets[n, 0] lies in 0 .. 512 and nest_offsets[n, 1] in 0 .. 1023. priority[x, y] is -1 or a nest n with nest_offsets[n, 0] <= y < nest_offsets[n, 0] + 512.
All inputs are finite; a program needn't handle non-finite values.
Results may differ from a plain program's by a relative error of at most 0.000058.
Values sent between devices are 32-bit elements; how exact they have to be, the bound alone decides.
A program may use at most 128 MiB of HBM per device.

v0:
```python
import functools

import jax
import jax.numpy as jnp
from jax import lax
from jax.experimental import pallas as pl
from jax.experimental.pallas import tpu as pltpu
from jax.sharding import PartitionSpec as P

MESH = pl.DeviceIdType.MESH
LANES = 128
F32 = jnp.float32
BF16 = jnp.bfloat16


def split(value):
    high = value.astype(BF16)
    return high, (value - high.astype(F32)).astype(BF16)


def dot(a, b):
    return jnp.dot(a, b, preferred_element_type=F32)


def remote(src, dst, send_sem, recv_sem, where):
    return pltpu.make_async_remote_copy(
        src_ref=src,
        dst_ref=dst,
        send_sem=send_sem,
        recv_sem=recv_sem,
        device_id=where,
        device_id_type=MESH,
    )


def order(groups):
    for g in range(groups):
        yield "R", g
        yield "S", g
    for g in range(groups + 3):
        if g < groups:
            yield "F", g
        if 0 <= g - 1 < groups:
            yield "M", g - 1
        if 0 <= g - 2 < groups:
            yield "E", g - 2


def kernel(
    tiles,
    nests,
    offs_ref,
    rate_ref,
    rw_hbm,
    prio_hbm,
    child_hbm,
    cw_hbm,
    parent_hbm,
    result,
    rw_ref,
    prio_ref,
    child,
    cw,
    cw_high,
    cw_low,
    merged,
    pieces,
    strips,
    blocks,
    slabs,
    ew_out,
    ew_in,
    ns_out,
    ns_in,
    small_sem,
    child_sem,
    cw_sem,
    parent_sem,
    a2a_send,
    a2a_recv,
    slab_send,
    slab_recv,
    edge_send,
    edge_recv,
):
    planes, crow, ccols = child.shape
    prd = rw_ref.shape[0]
    cols, rows = prio_ref.shape
    per = LANES // cols
    groups = planes // per
    nrows = prd * tiles
    m = per * prd
    me_n, me_t = lax.axis_index("nest"), lax.axis_index("tile")

    def group(ref, g):
        return ref.at[pl.ds(g * per, per)]

    child_in = [
        pltpu.make_async_copy(group(child_hbm.at[0], g), group(child, g), child_sem.at[g])
        for g in range(groups)
    ]
    chunks = cw_sem.shape[0]
    depth = ccols // chunks
    cw_in = [
        pltpu.make_async_copy(
            cw_hbm.at[pl.ds(k * depth, depth)], cw.at[pl.ds(k * depth, depth)], cw_sem.at[k]
        )
        for k in range(chunks)
    ]
    parent_in = pltpu.make_async_copy(parent_hbm, merged, parent_sem)
    rw_in = pltpu.make_async_copy(rw_hbm, rw_ref, small_sem.at[0])
    prio_in = pltpu.make_async_copy(prio_hbm, prio_ref, small_sem.at[1])
    rw_in.start()
    child_in[0].start()
    for k in range(chunks):
        cw_in[k].start()
    for g in range(1, groups):
        child_in[g].start()
    prio_in.start()
    parent_in.start()
    barrier = pltpu.get_barrier_semaphore()
    for d in range(1, tiles):
        pl.semaphore_signal(
            barrier, inc=1, device_id={"tile": lax.rem(me_t + d, tiles)}, device_id_type=MESH
        )
    for d in range(1, nests):
        pl.semaphore_signal(
            barrier, inc=1, device_id={"nest": lax.rem(me_n + d, nests)}, device_id_type=MESH
        )

    rw_in.wait()
    rw = rw_ref[...]
    spread_rows = lax.broadcasted_iota(jnp.int32, (per * crow, crow), 0)
    spread_cols = lax.broadcasted_iota(jnp.int32, (per * crow, crow), 1)
    spread = jnp.where(lax.rem(spread_rows, crow) == spread_cols, 1.0, 0.0).astype(BF16)
    wide_r = lax.broadcasted_iota(jnp.int32, (m, per * crow), 0)
    wide_c = lax.broadcasted_iota(jnp.int32, (m, per * crow), 1)
    diagonal = wide_r // prd == wide_c // crow
    block_rw = []
    for part in split(rw):
        line = lax.dot_general(
            part, spread, (((1,), (1,)), ((), ())), preferred_element_type=F32
        )
        line = jnp.concatenate([line] * per, axis=0)
        block_rw.append(jnp.where(diagonal, line, 0.0).astype(BF16))
    both_rw = jnp.concatenate(block_rw, axis=0)

    lane_group = lax.broadcasted_iota(jnp.int32, (prd, LANES), 1) // cols
    left, top = jnp.int32(0), jnp.int32(0)
    for n in range(nests):
        left = jnp.where(me_n == n, offs_ref[1, n], left)
        top = jnp.where(me_n == n, offs_ref[0, n], top)
    top = lax.rem(top, nrows)

    here = pl.ds(pl.multiple_of(me_t * prd, prd), prd)

    def fold(both, high, b_high, b_low):
        wide = dot(both, b_high)
        return (wide[:m] + wide[m:]) + dot(high, b_low)

    def restrict(g):
        child_in[g].wait()
        block = child[g * per : (g + 1) * per].reshape(per * crow, ccols)
        thinned = fold(both_rw, block_rw[0], *split(block))
        high, low = split(thinned)
        both = jnp.concatenate([high, low], axis=0)
        if g == 0:
            restricted = None
            for k in range(chunks):
                part = slice(k * depth, (k + 1) * depth)
                cw_in[k].wait()
                w_high, w_low = split(cw[part])
                cw_high[part] = w_high
                cw_low[part] = w_low
                now = fold(both[:, part], high[:, part], w_high, w_low)
                restricted = now if k == 0 else restricted + now
        else:
            restricted = fold(both, high, cw_high[...], cw_low[...])
        restricted = pltpu.roll(restricted, left, 1)
        for t in range(tiles):
            base, off = (t * cols) // LANES * LANES, (t * cols) % LANES
            piece = None
            for j in range(per):
                part = restricted[j * prd : (j + 1) * prd, base : base + LANES]
                shift = (j * cols - off) % LANES
                if shift:
                    part = pltpu.roll(part, shift, 1)
                piece = part if j == 0 else jnp.where(lane_group == j, part, piece)
            pieces[g, t] = piece
        strips[g, here, :] = pieces[g, me_t]

    def send(g):
        if g == 0:
            pl.semaphore_wait(barrier, tiles + nests - 2)
        for d in range(1, tiles):
            t = lax.rem(me_t + d, tiles)
            remote(
                pieces.at[g, t],
                strips.at[g, here, :],
                a2a_send.at[g],
                a2a_recv.at[g],
                {"tile": t},
            ).start()

    def a2a_bytes(g):
        most = strips.at[g, pl.ds(0, prd * (tiles - 1)), :]
        return remote(most, most, a2a_send.at[g], a2a_recv.at[g], {"tile": me_t})

    slab_out = []

    def forward(g):
        a2a_bytes(g).wait_recv()
        turned = pltpu.roll(strips[g].T, top, 1)
        for b in range(nrows // rows):
            blocks[g, b] = turned[:, b * rows : (b + 1) * rows]
        for d in range(1, nests):
            to = lax.rem(me_n + d, nests)
            copy = remote(
                blocks.at[g, lax.rem(to, nrows // rows)],
                slabs.at[g, d - 1],
                slab_send.at[g, d - 1],
                slab_recv.at[g, d - 1],
                {"nest": to},
            )
            copy.start()
            slab_out.append(copy)

    prio_in.wait()
    prio = prio_ref[...]
    west_t, east_t = lax.rem(me_t + tiles - 1, tiles), lax.rem(me_t + 1, tiles)
    low_n, high_n = lax.rem(me_n + nests - 1, nests), lax.rem(me_n + 1, nests)
    lane = lax.broadcasted_iota(jnp.int32, (cols, LANES), 1)

    edges = {}

    def merge(g):
        if g == 0:
            parent_in.wait()
        now = merged[g * per : (g + 1) * per]
        mine = blocks[g, lax.rem(me_n, nrows // rows)].reshape(per, cols, rows)
        now = jnp.where((prio == me_n)[None], mine, now)
        for d in range(1, nests):
            slab_out[g * (nests - 1) + d - 1].wait_recv()
            there = lax.rem(me_n + nests - d, nests)
            now = jnp.where((prio == there)[None], slabs[g, d - 1].reshape(per, cols, rows), now)
        merged[g * per : (g + 1) * per] = now
        low = jnp.zeros((cols, LANES), F32)
        high = jnp.zeros((cols, LANES), F32)
        for j in range(per):
            low = jnp.where(lane == j, now[j, :, :1], low)
            high = jnp.where(lane == j, now[j, :, rows - 1 :], high)
            ew_out[g, 0, j : j + 1] = now[j, :1]
            ew_out[g, 1, j : j + 1] = now[j, cols - 1 :]
        ns_out[g, 0] = low
        ns_out[g, 1] = high
        for side, (source, target, where) in enumerate(
            (
                (ew_out.at[g, 0], ew_in.at[g, 0], {"tile": west_t}),
                (ew_out.at[g, 1], ew_in.at[g, 1], {"tile": east_t}),
                (ns_out.at[g, 0], ns_in.at[g, 0], {"nest": low_n}),
                (ns_out.at[g, 1], ns_in.at[g, 1], {"nest": high_n}),
            )
        ):
            copy = remote(source, target, edge_send.at[g, side], edge_recv.at[g, side], where)
            copy.start()
            edges[g, side] = copy

    row_lane = lax.broadcasted_iota(jnp.int32, (cols, rows), 1)

    def finish(g):
        for side in range(4):
            edges[g, side].wait_recv()
        for j in range(per):
            f = g * per + j
            now = merged[f]
            east = jnp.concatenate([now[1:], ew_in[g, 0, j : j + 1]], axis=0)
            west = jnp.concatenate([ew_in[g, 1, j : j + 1], now[:-1]], axis=0)
            above = jnp.where(me_n == nests - 1, now[:, rows - 1 :], ns_in[g, 0, :, j : j + 1])
            below = jnp.where(me_n == 0, now[:, :1], ns_in[g, 1, :, j : j + 1])
            north = jnp.where(row_lane == rows - 1, above, pltpu.roll(now, rows - 1, 1))
            south = jnp.where(row_lane == 0, below, pltpu.roll(now, 1, 1))
            result[f] = now + rate_ref[f] * (east + west + north + south - 4.0 * now)

    stages = {"R": restrict, "S": send, "F": forward, "M": merge, "E": finish}
    for step in order(groups):
        stages[step[0]](step[1])

    for g in range(groups):
        a2a_bytes(g).wait_send()
    for copy in slab_out + list(edges.values()):
        copy.wait_send()


def per_device(
    child_fields, row_weights, col_weights, nest_offsets, priority, parent_old, smooth_rate
):
    planes, crow, ccols = child_fields.shape[1:]
    prd = row_weights.shape[0]
    _, cols, rows = parent_old.shape
    tiles, nests = lax.axis_size("tile"), lax.axis_size("nest")
    per = LANES // cols
    groups = planes // per
    nrows = prd * tiles
    smem = pl.BlockSpec(memory_space=pltpu.SMEM)
    hbm = pl.BlockSpec(memory_space=pl.ANY)
    dma = pltpu.SemaphoreType.DMA
    return pl.pallas_call(
        functools.partial(kernel, tiles, nests),
        out_shape=pltpu.VMEM(parent_old.shape, F32),
        in_specs=[smem, smem] + [hbm] * 5,
        out_specs=pl.BlockSpec(memory_space=pltpu.VMEM),
        scratch_shapes=[
            pltpu.VMEM(row_weights.shape, F32),
            pltpu.VMEM((cols, rows), jnp.int32),
            pltpu.VMEM((planes, crow, ccols), F32),
            pltpu.VMEM(col_weights.shape, F32),
            pltpu.VMEM(col_weights.shape, BF16),
            pltpu.VMEM(col_weights.shape, BF16),
            pltpu.VMEM((planes, cols, rows), F32),
            pltpu.VMEM((groups, tiles, prd, LANES), F32),
            pltpu.VMEM((groups, nrows, LANES), F32),
            pltpu.VMEM((groups, nrows // rows, LANES, rows), F32),
            pltpu.VMEM((groups, nests - 1, LANES, rows), F32),
            pltpu.VMEM((groups, 2, per, rows), F32),
            pltpu.VMEM((groups, 2, per, rows), F32),
            pltpu.VMEM((groups, 2, cols, LANES), F32),
            pltpu.VMEM((groups, 2, cols, LANES), F32),
            dma((2,)),
            dma((groups,)),
            dma((6,)),
            dma,
            dma((groups,)),
            dma((groups,)),
            dma((groups, nests - 1)),
            dma((groups, nests - 1)),
            dma((groups, 4)),
            dma((groups, 4)),
        ],
        compiler_params=pltpu.CompilerParams(
            collective_id=0, has_side_effects=True, vmem_limit_bytes=60 * 2**20
        ),
    )(nest_offsets.T, smooth_rate, row_weights, priority, child_fields, col_weights, parent_old)


def solution(mesh):
    return jax.shard_map(
        per_device,
        mesh=mesh,
        in_specs=(
            P("nest", None, "tile", None),
            P(),
            P(),
            P(),
            P("tile", "nest"),
            P(None, "tile", "nest"),
            P(),
        ),
        out_specs=P(None, "tile", "nest"),
        check_vma=False,
    )
```

profile of v0, /device:TPU:1, one launch (start us, length us, event | category | flops | bytes accessed | tf_op | source)
XLA Modules:
  0.0 59.7 jit_solution(14384387032755123833)
XLA Ops:
  0.0 58.9 %shard_map.73 = f32[32,16,256]{2,1,0:T(8,128)S(1)} custom-call(s32[2,4]{1,0:T(2,128)} %bitcast.1, f32[32]{0:T(128)} %rate_ref.1, f32[8,24]{1,0:T(8,128)} %rw_hbm.1, s32[16,256]{1,0:T(8,128)} %prio_hbm.1, f32[1,32,24,3072]{3,2,1,0:T(8,128)} %child_hbm.1, f32[3072,1024]{1,0:T(8,128)} %cw_hbm.1, f32[32,16,256]{2,1,0:T(8,128)} %parent_hbm.1), custom_call_target="tpu_custom_call" | custom-call | tf_op jit(solution)/shard_map/pallas_call | solution.py:307
  58.9 0.8 %copy.9 = f32[32,16,256]{2,1,0:T(8,128)} copy(f32[32,16,256]{2,1,0:T(8,128)S(1)} %shard_map.73) | data formatting | bytes 1048576
where the time goes:
time: 59.8 us; the launch traced here: 59.7 us
  Pallas kernels  58.9 us (98%)
  local copies, waits for them, and re-layouts  0.8 us (1%)
    pallas_call x1, Pallas kernels, per_device(): pl.pallas_call(functools.partial(kernel, tiles, nests), out_shape=pltpu.V...  58.9 us

commit v1 on v0

--- a/solution.py
+++ b/solution.py
@@ -11,6 +11,8 @@
 LANES = 128
 F32 = jnp.float32
 BF16 = jnp.bfloat16
+CHUNKS = 6
+AHEAD = 3
 
 
 def split(value):
@@ -34,9 +36,6 @@
 
 
 def order(groups):
-    for g in range(groups):
-        yield "R", g
-        yield "S", g
     for g in range(groups + 3):
         if g < groups:
             yield "F", g
@@ -49,20 +48,24 @@
 def kernel(
     tiles,
     nests,
-    offs_ref,
-    rate_ref,
+    offs_hbm,
+    rate_hbm,
     rw_hbm,
     prio_hbm,
     child_hbm,
     cw_hbm,
     parent_hbm,
     result,
+    offs_ref,
+    rate_ref,
     rw_ref,
     prio_ref,
     child,
     cw,
     cw_high,
     cw_low,
+    both_ref,
+    restricted_ref,
     merged,
     pieces,
     strips,
@@ -92,37 +95,38 @@
     m = per * prd
     me_n, me_t = lax.axis_index("nest"), lax.axis_index("tile")
 
-    def group(ref, g):
-        return ref.at[pl.ds(g * per, per)]
-
-    child_in = [
-        pltpu.make_async_copy(group(child_hbm.at[0], g), group(child, g), child_sem.at[g])
-        for g in range(groups)
-    ]
+    def child_in(g):
+        fields = pl.ds(g * per, per)
+        return pltpu.make_async_copy(child_hbm.at[0, fields], child.at[fields], child_sem.at[g])
+
     chunks = cw_sem.shape[0]
     depth = ccols // chunks
-    cw_in = [
-        pltpu.make_async_copy(
-            cw_hbm.at[pl.ds(k * depth, depth)], cw.at[pl.ds(k * depth, depth)], cw_sem.at[k]
-        )
-        for k in range(chunks)
-    ]
+
+    def cw_in(k):
+        part = pl.ds(pl.multiple_of(k * depth, depth), depth)
+        return pltpu.make_async_copy(cw_hbm.at[part], cw.at[part], cw_sem.at[k])
+
     parent_in = pltpu.make_async_copy(parent_hbm, merged, parent_sem)
     rw_in = pltpu.make_async_copy(rw_hbm, rw_ref, small_sem.at[0])
     prio_in = pltpu.make_async_copy(prio_hbm, prio_ref, small_sem.at[1])
+    offs_in = pltpu.make_async_copy(offs_hbm, offs_ref, small_sem.at[2])
+    rate_in = pltpu.make_async_copy(rate_hbm, rate_ref, small_sem.at[3])
     rw_in.start()
-    child_in[0].start()
-    for k in range(chunks):
-        cw_in[k].start()
-    for g in range(1, groups):
-        child_in[g].start()
+    child_in(0).start()
+    for k in range(AHEAD):
+        cw_in(k).start()
+    offs_in.start()
+    rate_in.start()
     prio_in.start()
-    parent_in.start()
     barrier = pltpu.get_barrier_semaphore()
-    for d in range(1, tiles):
+
+    def greet_tile(d, carry):
         pl.semaphore_signal(
             barrier, inc=1, device_id={"tile": lax.rem(me_t + d, tiles)}, device_id_type=MESH
         )
+        return carry
+
+    lax.fori_loop(1, tiles, greet_tile, 0)
     for d in range(1, nests):
         pl.semaphore_signal(
             barrier, inc=1, device_id={"nest": lax.rem(me_n + d, nests)}, device_id_type=MESH
@@ -146,6 +150,8 @@
     both_rw = jnp.concatenate(block_rw, axis=0)
 
     lane_group = lax.broadcasted_iota(jnp.int32, (prd, LANES), 1) // cols
+    offs_in.wait()
+    rate_in.wait()
     left, top = jnp.int32(0), jnp.int32(0)
     for n in range(nests):
         left = jnp.where(me_n == n, offs_ref[1, n], left)
@@ -158,41 +164,34 @@
         wide = dot(both, b_high)
         return (wide[:m] + wide[m:]) + dot(high, b_low)
 
-    def restrict(g):
-        child_in[g].wait()
-        block = child[g * per : (g + 1) * per].reshape(per * crow, ccols)
+    def thin(g):
+        child_in(g).wait()
+        block = child[pl.ds(g * per, per)].reshape(per * crow, ccols)
         thinned = fold(both_rw, block_rw[0], *split(block))
         high, low = split(thinned)
-        both = jnp.concatenate([high, low], axis=0)
-        if g == 0:
-            restricted = None
-            for k in range(chunks):
-                part = slice(k * depth, (k + 1) * depth)
-                cw_in[k].wait()
-                w_high, w_low = split(cw[part])
-                cw_high[part] = w_high
-                cw_low[part] = w_low
-                now = fold(both[:, part], high[:, part], w_high, w_low)
-                restricted = now if k == 0 else restricted + now
-        else:
-            restricted = fold(both, high, cw_high[...], cw_low[...])
-        restricted = pltpu.roll(restricted, left, 1)
-        for t in range(tiles):
-            base, off = (t * cols) // LANES * LANES, (t * cols) % LANES
-            piece = None
-            for j in range(per):
-                part = restricted[j * prd : (j + 1) * prd, base : base + LANES]
-                shift = (j * cols - off) % LANES
-                if shift:
-                    part = pltpu.roll(part, shift, 1)
-                piece = part if j == 0 else jnp.where(lane_group == j, part, piece)
-            pieces[g, t] = piece
+        both_ref[:m] = high
+        both_ref[m:] = low
+
+    def cut(g):
+        restricted = pltpu.roll(restricted_ref[...], left, 1)
+        for base in range(0, tiles * cols, LANES):
+            parts = [restricted[j * prd : (j + 1) * prd, base : base + LANES] for j in range(per)]
+            step = per // 2
+            while step:
+                for a in range(per):
+                    if a & step:
+                        continue
+                    one, two = parts[a], parts[a + step]
+                    keep = lane_group & step == 0
+                    parts[a] = jnp.where(keep, one, pltpu.roll(two, step * cols, 1))
+                    parts[a + step] = jnp.where(keep, pltpu.roll(one, LANES - step * cols, 1), two)
+                step //= 2
+            for q in range(per):
+                pieces[g, base // cols + q] = parts[q]
         strips[g, here, :] = pieces[g, me_t]
 
     def send(g):
-        if g == 0:
-            pl.semaphore_wait(barrier, tiles + nests - 2)
-        for d in range(1, tiles):
+        def send_one(d, carry):
             t = lax.rem(me_t + d, tiles)
             remote(
                 pieces.at[g, t],
@@ -201,6 +200,36 @@
                 a2a_recv.at[g],
                 {"tile": t},
             ).start()
+            return carry
+
+        lax.fori_loop(1, tiles, send_one, 0)
+
+    def first():
+        thin(0)
+        for k in range(chunks):
+            part = slice(k * depth, (k + 1) * depth)
+            cw_in(k).wait()
+            if k + AHEAD < chunks:
+                cw_in(k + AHEAD).start()
+            for g in range(1, groups):
+                if k == min(chunks - AHEAD + g - 1, chunks - 1):
+                    child_in(g).start()
+            w_high, w_low = split(cw[part])
+            cw_high[part] = w_high
+            cw_low[part] = w_low
+            now = fold(both_ref[:, part], both_ref[:m, part], w_high, w_low)
+            restricted_ref[...] = now if k == 0 else restricted_ref[...] + now
+        cut(0)
+        parent_in.start()
+        pl.semaphore_wait(barrier, tiles + nests - 2)
+        send(0)
+
+    def restrict(g, carry):
+        thin(g)
+        restricted_ref[...] = fold(both_ref[...], both_ref[:m], cw_high[...], cw_low[...])
+        cut(g)
+        send(g)
+        return carry
 
     def a2a_bytes(g):
         most = strips.at[g, pl.ds(0, prd * (tiles - 1)), :]
@@ -281,7 +310,9 @@
             south = jnp.where(row_lane == 0, below, pltpu.roll(now, 1, 1))
             result[f] = now + rate_ref[f] * (east + west + north + south - 4.0 * now)
 
-    stages = {"R": restrict, "S": send, "F": forward, "M": merge, "E": finish}
+    first()
+    lax.fori_loop(1, groups, restrict, 0)
+    stages = {"F": forward, "M": merge, "E": finish}
     for step in order(groups):
         stages[step[0]](step[1])
 
@@ -301,21 +332,24 @@
     per = LANES // cols
     groups = planes // per
     nrows = prd * tiles
-    smem = pl.BlockSpec(memory_space=pltpu.SMEM)
     hbm = pl.BlockSpec(memory_space=pl.ANY)
     dma = pltpu.SemaphoreType.DMA
     return pl.pallas_call(
         functools.partial(kernel, tiles, nests),
         out_shape=pltpu.VMEM(parent_old.shape, F32),
-        in_specs=[smem, smem] + [hbm] * 5,
+        in_specs=[hbm] * 7,
         out_specs=pl.BlockSpec(memory_space=pltpu.VMEM),
         scratch_shapes=[
+            pltpu.SMEM((2, nests), jnp.int32),
+            pltpu.SMEM((planes,), F32),
             pltpu.VMEM(row_weights.shape, F32),
             pltpu.VMEM((cols, rows), jnp.int32),
             pltpu.VMEM((planes, crow, ccols), F32),
             pltpu.VMEM(col_weights.shape, F32),
             pltpu.VMEM(col_weights.shape, BF16),
             pltpu.VMEM(col_weights.shape, BF16),
+            pltpu.VMEM((2 * per * prd, ccols), BF16),
+            pltpu.VMEM((per * prd, col_weights.shape[1]), F32),
             pltpu.VMEM((planes, cols, rows), F32),
             pltpu.VMEM((groups, tiles, prd, LANES), F32),
             pltpu.VMEM((groups, nrows, LANES), F32),
@@ -325,9 +359,9 @@
             pltpu.VMEM((groups, 2, per, rows), F32),
             pltpu.VMEM((groups, 2, cols, LANES), F32),
             pltpu.VMEM((groups, 2, cols, LANES), F32),
-            dma((2,)),
+            dma((4,)),
             dma((groups,)),
-            dma((6,)),
+            dma((CHUNKS,)),
             dma,
             dma((groups,)),
             dma((groups,)),

time: 59.8 us -> 56.5 us (0.945)
  Pallas kernels: 58.9 us -> 55.4 us
    pallas_call x1, Pallas kernels: 58.9 us -> 55.4 us  [per_device(): pl.pallas_call(functools.partial(kernel, tiles, nests), out_shape=pltpu.V...]
where the time goes in v1:
time: 56.5 us; the launch traced here: 56.2 us
  Pallas kernels  55.4 us (98%)
  local copies, waits for them, and re-layouts  0.8 us (1%)
    pallas_call x1, Pallas kernels, per_device(): pl.pallas_call(functools.partial(kernel, tiles, nests), out_shape=pltpu.V...  55.4 us

profile of v1, /device:TPU:1, one launch (start us, length us, event | category | flops | bytes accessed | tf_op | source)
XLA Modules:
  0.0 56.2 jit_solution(2335180265117770931)
XLA Ops:
  0.0 55.4 %shard_map.73 = f32[32,16,256]{2,1,0:T(8,128)S(1)} custom-call(s32[2,4]{1,0:T(2,128)} %bitcast.1, f32[32]{0:T(128)} %rate_hbm.1, f32[8,24]{1,0:T(8,128)} %rw_hbm.1, s32[16,256]{1,0:T(8,128)} %prio_hbm.1, f32[1,32,24,3072]{3,2,1,0:T(8,128)} %child_hbm.1, f32[3072,1024]{1,0:T(8,128)} %cw_hbm.1, f32[32,16,256]{2,1,0:T(8,128)} %parent_hbm.1), custom_call_target="tpu_custom_call" | custom-call | tf_op jit(solution)/shard_map/pallas_call | solution.py:337
  55.4 0.8 %copy.9 = f32[32,16,256]{2,1,0:T(8,128)} copy(f32[32,16,256]{2,1,0:T(8,128)S(1)} %shard_map.73) | data formatting | bytes 1048576

commit v2 on v1

--- a/solution.py
+++ b/solution.py
@@ -13,6 +13,7 @@
 BF16 = jnp.bfloat16
 CHUNKS = 6
 AHEAD = 3
+SPAN = 2
 
 
 def split(value):
@@ -36,13 +37,15 @@
 
 
 def order(groups):
-    for g in range(groups + 3):
+    for g in range(groups + 2):
         if g < groups:
             yield "F", g
         if 0 <= g - 1 < groups:
             yield "M", g - 1
         if 0 <= g - 2 < groups:
             yield "E", g - 2
+        if g < groups:
+            yield "P", g
 
 
 def kernel(
@@ -70,7 +73,10 @@
     pieces,
     strips,
     blocks,
+    via,
+    relayed,
     slabs,
+    prio_near,
     ew_out,
     ew_in,
     ns_out,
@@ -81,6 +87,10 @@
     parent_sem,
     a2a_send,
     a2a_recv,
+    near_send,
+    near_recv,
+    via_send,
+    via_recv,
     slab_send,
     slab_recv,
     edge_send,
@@ -165,7 +175,6 @@
         return (wide[:m] + wide[m:]) + dot(high, b_low)
 
     def thin(g):
-        child_in(g).wait()
         block = child[pl.ds(g * per, per)].reshape(per * crow, ccols)
         thinned = fold(both_rw, block_rw[0], *split(block))
         high, low = split(thinned)
@@ -205,15 +214,18 @@
         lax.fori_loop(1, tiles, send_one, 0)
 
     def first():
+        child_in(0).wait()
+        cw_in(AHEAD).start()
         thin(0)
-        for k in range(chunks):
-            part = slice(k * depth, (k + 1) * depth)
-            cw_in(k).wait()
-            if k + AHEAD < chunks:
-                cw_in(k + AHEAD).start()
-            for g in range(1, groups):
-                if k == min(chunks - AHEAD + g - 1, chunks - 1):
-                    child_in(g).start()
+        for k in range(0, chunks, SPAN):
+            part = slice(k * depth, (k + SPAN) * depth)
+            for c in range(k, k + SPAN):
+                cw_in(c).wait()
+                if c + AHEAD + 1 < chunks:
+                    cw_in(c + AHEAD + 1).start()
+                for g in range(1, groups):
+                    if c == min(chunks - AHEAD - 2 + g, chunks - 1):
+                        child_in(g).start()
             w_high, w_low = split(cw[part])
             cw_high[part] = w_high
             cw_low[part] = w_low
@@ -222,9 +234,11 @@
         cut(0)
         parent_in.start()
         pl.semaphore_wait(barrier, tiles + nests - 2)
+        swap_priorities()
         send(0)
 
     def restrict(g, carry):
+        child_in(g).wait()
         thin(g)
         restricted_ref[...] = fold(both_ref[...], both_ref[:m], cw_high[...], cw_low[...])
         cut(g)
@@ -235,30 +249,56 @@
         most = strips.at[g, pl.ds(0, prd * (tiles - 1)), :]
         return remote(most, most, a2a_send.at[g], a2a_recv.at[g], {"tile": me_t})
 
-    slab_out = []
+    prio_in.wait()
+    prio = prio_ref[...]
+    west_t, east_t = lax.rem(me_t + tiles - 1, tiles), lax.rem(me_t + 1, tiles)
+    low_n, high_n = lax.rem(me_n + nests - 1, nests), lax.rem(me_n + 1, nests)
+    lane = lax.broadcasted_iota(jnp.int32, (cols, LANES), 1)
+
+    near = lax.rem(me_n + 1, 2)
+    half = LANES // 2
+    halves = pl.ds(0, half), pl.ds(half, half)
+    sent = {}
+
+    def pass_on(key, source, target, sems, to):
+        copy = remote(source, target, *sems, {"nest": to})
+        copy.start()
+        sent[key] = copy
+
+    def swap_priorities():
+        for side, to in enumerate((high_n, low_n)):
+            sems = near_send.at[side], near_recv.at[side]
+            pass_on(("prio", side), prio_ref, prio_near.at[side], sems, to)
 
     def forward(g):
         a2a_bytes(g).wait_recv()
         turned = pltpu.roll(strips[g].T, top, 1)
         for b in range(nrows // rows):
             blocks[g, b] = turned[:, b * rows : (b + 1) * rows]
-        for d in range(1, nests):
-            to = lax.rem(me_n + d, nests)
-            copy = remote(
-                blocks.at[g, lax.rem(to, nrows // rows)],
-                slabs.at[g, d - 1],
-                slab_send.at[g, d - 1],
-                slab_recv.at[g, d - 1],
-                {"nest": to},
-            )
-            copy.start()
-            slab_out.append(copy)
-
-    prio_in.wait()
-    prio = prio_ref[...]
-    west_t, east_t = lax.rem(me_t + tiles - 1, tiles), lax.rem(me_t + 1, tiles)
-    low_n, high_n = lax.rem(me_n + nests - 1, nests), lax.rem(me_n + 1, nests)
-    lane = lax.broadcasted_iota(jnp.int32, (cols, LANES), 1)
+        for side, to in enumerate((high_n, low_n)):
+            source = blocks.at[g, 1 - near, halves[side]]
+            sems = via_send.at[g, side], via_recv.at[g, side]
+            pass_on(("via", g, side), source, via.at[g, side], sems, to)
+        for side, to in enumerate((high_n, low_n)):
+            part = halves[1 - side]
+            sems = slab_send.at[g, side], slab_recv.at[g, side]
+            source = blocks.at[g, near, part]
+            pass_on(("slab", g, side), source, slabs.at[g, side, part], sems, to)
+
+    def relay(g):
+        if g == 0:
+            for side in range(2):
+                sent["prio", side].wait_recv()
+        for side, to in enumerate((high_n, low_n)):
+            sent["via", g, side].wait_recv()
+            origin = (low_n, high_n)[side]
+            theirs = (prio_near[1 - side] == origin)[None]
+            far = via[g, side].reshape(per // 2, cols, rows)
+            own = blocks[g, near, side * half : (side + 1) * half].reshape(per // 2, cols, rows)
+            relayed[g, side] = jnp.where(theirs, far, own).reshape(half, rows)
+            sems = slab_send.at[g, 2 + side], slab_recv.at[g, 2 + side]
+            target = slabs.at[g, side, halves[side]]
+            pass_on(("slab", g, 2 + side), relayed.at[g, side], target, sems, to)
 
     edges = {}
 
@@ -268,10 +308,20 @@
         now = merged[g * per : (g + 1) * per]
         mine = blocks[g, lax.rem(me_n, nrows // rows)].reshape(per, cols, rows)
         now = jnp.where((prio == me_n)[None], mine, now)
-        for d in range(1, nests):
-            slab_out[g * (nests - 1) + d - 1].wait_recv()
-            there = lax.rem(me_n + nests - d, nests)
-            now = jnp.where((prio == there)[None], slabs[g, d - 1].reshape(per, cols, rows), now)
+        for q in range(4):
+            sent["slab", g, q].wait_recv()
+        far_n = lax.rem(me_n + 2, nests)
+        ways = [(prio == n)[None] for n in (low_n, high_n)]
+        far = (prio == far_n)[None]
+        mixed = []
+        for side in range(2):
+            part = now[side * (per // 2) : (side + 1) * (per // 2)]
+            for way in range(2):
+                take = (ways[way] | far) if way == side else ways[way]
+                slab = slabs[g, way, side * half : (side + 1) * half]
+                part = jnp.where(take, slab.reshape(per // 2, cols, rows), part)
+            mixed.append(part)
+        now = jnp.concatenate(mixed, axis=0)
         merged[g * per : (g + 1) * per] = now
         low = jnp.zeros((cols, LANES), F32)
         high = jnp.zeros((cols, LANES), F32)
@@ -312,13 +362,13 @@
 
     first()
     lax.fori_loop(1, groups, restrict, 0)
-    stages = {"F": forward, "M": merge, "E": finish}
+    stages = {"F": forward, "P": relay, "M": merge, "E": finish}
     for step in order(groups):
         stages[step[0]](step[1])
 
     for g in range(groups):
         a2a_bytes(g).wait_send()
-    for copy in slab_out + list(edges.values()):
+    for copy in [*sent.values(), *edges.values()]:
         copy.wait_send()
 
 
@@ -354,7 +404,10 @@
             pltpu.VMEM((groups, tiles, prd, LANES), F32),
             pltpu.VMEM((groups, nrows, LANES), F32),
             pltpu.VMEM((groups, nrows // rows, LANES, rows), F32),
-            pltpu.VMEM((groups, nests - 1, LANES, rows), F32),
+            pltpu.VMEM((groups, 2, LANES // 2, rows), F32),
+            pltpu.VMEM((groups, 2, LANES // 2, rows), F32),
+            pltpu.VMEM((groups, 2, LANES, rows), F32),
+            pltpu.VMEM((2, cols, rows), jnp.int32),
             pltpu.VMEM((groups, 2, per, rows), F32),
             pltpu.VMEM((groups, 2, per, rows), F32),
             pltpu.VMEM((groups, 2, cols, LANES), F32),
@@ -365,8 +418,12 @@
             dma,
             dma((groups,)),
             dma((groups,)),
-            dma((groups, nests - 1)),
-            dma((groups, nests - 1)),
+            dma((2,)),
+            dma((2,)),
+            dma((groups, 2)),
+            dma((groups, 2)),
+            dma((groups, 4)),
+            dma((groups, 4)),
             dma((groups, 4)),
             dma((groups, 4)),
         ],

time: 56.5 us -> 55.4 us (0.981)
  Pallas kernels: 55.4 us -> 54.2 us
    pallas_call x1, Pallas kernels: 55.4 us -> 54.2 us  [per_device(): pl.pallas_call(functools.partial(kernel, tiles, nests), out_shape=pltpu.V...]
where the time goes in v2:
time: 55.4 us; the launch traced here: 55 us
  Pallas kernels  54.2 us (98%)
  local copies, waits for them, and re-layouts  0.8 us (1%)
    pallas_call x1, Pallas kernels, per_device(): pl.pallas_call(functools.partial(kernel, tiles, nests), out_shape=pltpu.V...  54.2 us

profile of v2, /device:TPU:1, one launch (start us, length us, event | category | flops | bytes accessed | tf_op | source)
XLA Modules:
  0.0 55.0 jit_solution(5623185396809440749)
XLA Ops:
  0.0 54.2 %shard_map.73 = f32[32,16,256]{2,1,0:T(8,128)S(1)} custom-call(s32[2,4]{1,0:T(2,128)} %bitcast.1, f32[32]{0:T(128)} %rate_hbm.1, f32[8,24]{1,0:T(8,128)} %rw_hbm.1, s32[16,256]{1,0:T(8,128)} %prio_hbm.1, f32[1,32,24,3072]{3,2,1,0:T(8,128)} %child_hbm.1, f32[3072,1024]{1,0:T(8,128)} %cw_hbm.1, f32[32,16,256]{2,1,0:T(8,128)} %parent_hbm.1), custom_call_target="tpu_custom_call" | custom-call | tf_op jit(solution)/shard_map/pallas_call | solution.py:387
  54.2 0.8 %copy.9 = f32[32,16,256]{2,1,0:T(8,128)} copy(f32[32,16,256]{2,1,0:T(8,128)S(1)} %shard_map.73) | data formatting | bytes 1048576

commit v3 on v2

--- a/solution.py
+++ b/solution.py
@@ -37,13 +37,11 @@
 
 
 def order(groups):
-    for g in range(groups + 2):
+    for g in range(groups + 1):
         if g < groups:
             yield "F", g
-        if 0 <= g - 1 < groups:
+        if g > 0:
             yield "M", g - 1
-        if 0 <= g - 2 < groups:
-            yield "E", g - 2
         if g < groups:
             yield "P", g
 
@@ -78,9 +76,12 @@
     slabs,
     prio_near,
     ew_out,
-    ew_in,
+    ew_old,
     ns_out,
-    ns_in,
+    ns_old,
+    ew_line,
+    ew_cand,
+    ns_cand,
     small_sem,
     child_sem,
     cw_sem,
@@ -95,6 +96,10 @@
     slab_recv,
     edge_send,
     edge_recv,
+    ew_send,
+    ew_recv,
+    ns_send,
+    ns_recv,
 ):
     planes, crow, ccols = child.shape
     prd = rw_ref.shape[0]
@@ -138,9 +143,11 @@
 
     lax.fori_loop(1, tiles, greet_tile, 0)
     for d in range(1, nests):
-        pl.semaphore_signal(
-            barrier, inc=1, device_id={"nest": lax.rem(me_n + d, nests)}, device_id_type=MESH
-        )
+        there = lax.rem(me_n + d, nests)
+        pl.semaphore_signal(barrier, inc=1, device_id={"nest": there}, device_id_type=MESH)
+        for step in (1, tiles - 1):
+            where = {"nest": there, "tile": lax.rem(me_t + step, tiles)}
+            pl.semaphore_signal(barrier, inc=1, device_id=where, device_id_type=MESH)
 
     rw_in.wait()
     rw = rw_ref[...]
@@ -233,7 +240,7 @@
             restricted_ref[...] = now if k == 0 else restricted_ref[...] + now
         cut(0)
         parent_in.start()
-        pl.semaphore_wait(barrier, tiles + nests - 2)
+        pl.semaphore_wait(barrier, tiles - 1 + 3 * (nests - 1))
         swap_priorities()
         send(0)
 
@@ -260,8 +267,9 @@
     halves = pl.ds(0, half), pl.ds(half, half)
     sent = {}
 
-    def pass_on(key, source, target, sems, to):
-        copy = remote(source, target, *sems, {"nest": to})
+    def pass_on(key, source, target, sems, to, tile=None):
+        where = {"nest": to} if tile is None else {"nest": to, "tile": tile}
+        copy = remote(source, target, *sems, where)
         copy.start()
         sent[key] = copy
 
@@ -269,6 +277,8 @@
         for side, to in enumerate((high_n, low_n)):
             sems = near_send.at[side], near_recv.at[side]
             pass_on(("prio", side), prio_ref, prio_near.at[side], sems, to)
+
+    strip_row = lax.broadcasted_iota(jnp.int32, (nrows, LANES), 0)
 
     def forward(g):
         a2a_bytes(g).wait_recv()
@@ -284,6 +294,26 @@
             sems = slab_send.at[g, side], slab_recv.at[g, side]
             source = blocks.at[g, near, part]
             pass_on(("slab", g, side), source, slabs.at[g, side, part], sems, to)
+        for side, col in enumerate((0, cols - 1)):
+            for j in range(per):
+                at = j * cols + col
+                for b in range(nrows // rows):
+                    ew_line[g, side, b, j : j + 1] = turned[at : at + 1, b * rows : (b + 1) * rows]
+        for q, residue in enumerate((nrows - 1, rows, rows - 1, 0)):
+            picked = strip_row == lax.rem(residue + nrows - top, nrows)
+            line = jnp.sum(jnp.where(picked, strips[g], 0.0), axis=0, keepdims=True)
+            ns_cand[g, q : q + 1] = line
+            ns_cand[g, q + 4 : q + 5] = line
+        for d in range(nests):
+            to = lax.rem(me_n + d, nests)
+            for side, tile in enumerate((west_t, east_t)):
+                source = ew_line.at[g, side, lax.rem(to, 2)]
+                sems = ew_send.at[g, side, d], ew_recv.at[g, side, d]
+                pass_on(("ew", g, side, d), source, ew_cand.at[g, side, d], sems, to, tile)
+            if d:
+                source, target = ns_cand.at[g, pl.ds(0, 8)], ns_cand.at[g, pl.ds(d * 8, 8)]
+                sems = ns_send.at[g, d - 1], ns_recv.at[g, d - 1]
+                pass_on(("ns", g, d), source, target, sems, to)
 
     def relay(g):
         if g == 0:
@@ -300,13 +330,33 @@
             target = slabs.at[g, side, halves[side]]
             pass_on(("slab", g, 2 + side), relayed.at[g, side], target, sems, to)
 
-    edges = {}
+    row_lane = lax.broadcasted_iota(jnp.int32, (cols, rows), 1)
+
+    def swap_edges():
+        parent_in.wait()
+        prio_f = prio.astype(F32)
+        for side, row in enumerate((0, rows - 1)):
+            line = jnp.zeros((cols, LANES), F32)
+            for f in range(planes):
+                line = jnp.where(lane == f, merged[f, :, row : row + 1], line)
+            ns_out[side] = jnp.where(lane == planes, prio_f[:, row : row + 1], line)
+            sems = edge_send.at[side], edge_recv.at[side]
+            to = (low_n, high_n)[side]
+            pass_on(("old", side), ns_out.at[side], ns_old.at[side], sems, to)
+        for side, col in enumerate((0, cols - 1)):
+            for f in range(planes):
+                ew_out[side, f : f + 1] = merged[f, col : col + 1]
+            ew_out[side, planes:] = jnp.broadcast_to(prio_f[col : col + 1], (8, rows))
+            sems = edge_send.at[2 + side], edge_recv.at[2 + side]
+            tile = (west_t, east_t)[side]
+            pass_on(("old", 2 + side), ew_out.at[side], ew_old.at[side], sems, me_n, tile)
 
     def merge(g):
         if g == 0:
-            parent_in.wait()
+            for side in range(4):
+                sent["old", side].wait_recv()
         now = merged[g * per : (g + 1) * per]
-        mine = blocks[g, lax.rem(me_n, nrows // rows)].reshape(per, cols, rows)
+        mine = blocks[g, 1 - near].reshape(per, cols, rows)
         now = jnp.where((prio == me_n)[None], mine, now)
         for q in range(4):
             sent["slab", g, q].wait_recv()
@@ -322,53 +372,54 @@
                 part = jnp.where(take, slab.reshape(per // 2, cols, rows), part)
             mixed.append(part)
         now = jnp.concatenate(mixed, axis=0)
-        merged[g * per : (g + 1) * per] = now
-        low = jnp.zeros((cols, LANES), F32)
-        high = jnp.zeros((cols, LANES), F32)
-        for j in range(per):
-            low = jnp.where(lane == j, now[j, :, :1], low)
-            high = jnp.where(lane == j, now[j, :, rows - 1 :], high)
-            ew_out[g, 0, j : j + 1] = now[j, :1]
-            ew_out[g, 1, j : j + 1] = now[j, cols - 1 :]
-        ns_out[g, 0] = low
-        ns_out[g, 1] = high
-        for side, (source, target, where) in enumerate(
-            (
-                (ew_out.at[g, 0], ew_in.at[g, 0], {"tile": west_t}),
-                (ew_out.at[g, 1], ew_in.at[g, 1], {"tile": east_t}),
-                (ns_out.at[g, 0], ns_in.at[g, 0], {"nest": low_n}),
-                (ns_out.at[g, 1], ns_in.at[g, 1], {"nest": high_n}),
-            )
-        ):
-            copy = remote(source, target, edge_send.at[g, side], edge_recv.at[g, side], where)
-            copy.start()
-            edges[g, side] = copy
-
-    row_lane = lax.broadcasted_iota(jnp.int32, (cols, rows), 1)
-
-    def finish(g):
-        for side in range(4):
-            edges[g, side].wait_recv()
+        origins = [lax.rem(me_n + nests - d, nests).astype(F32) for d in range(nests)]
+        beside = []
+        for side in range(2):
+            line = ew_old[side, g * per : (g + 1) * per]
+            owner = ew_old[side, planes:]
+            for d in range(nests):
+                sent["ew", g, side, d].wait_recv()
+                line = jnp.where(owner == origins[d], ew_cand[g, side, d], line)
+            beside.append(line)
+        for d in range(1, nests):
+            sent["ns", g, d].wait_recv()
+        lines = [
+            ns_cand[g, pl.ds(d * 8 + 2 * (1 - near) + way, 1), :]
+            for way in range(2)
+            for d in range(nests)
+        ]
+        lines.append(jnp.zeros((LANES - 2 * nests, LANES), F32))
+        ends = jnp.concatenate(lines, axis=0).T
         for j in range(per):
             f = g * per + j
-            now = merged[f]
-            east = jnp.concatenate([now[1:], ew_in[g, 0, j : j + 1]], axis=0)
-            west = jnp.concatenate([ew_in[g, 1, j : j + 1], now[:-1]], axis=0)
-            above = jnp.where(me_n == nests - 1, now[:, rows - 1 :], ns_in[g, 0, :, j : j + 1])
-            below = jnp.where(me_n == 0, now[:, :1], ns_in[g, 1, :, j : j + 1])
-            north = jnp.where(row_lane == rows - 1, above, pltpu.roll(now, rows - 1, 1))
-            south = jnp.where(row_lane == 0, below, pltpu.roll(now, 1, 1))
-            result[f] = now + rate_ref[f] * (east + west + north + south - 4.0 * now)
+            here_j = now[j]
+            outer = []
+            for way in range(2):
+                old = ns_old[1 - way]
+                cell, owner = old[:, f : f + 1], old[:, planes : planes + 1]
+                for d in range(nests):
+                    at = way * nests + d
+                    new = ends[j * cols : (j + 1) * cols, at : at + 1]
+                    cell = jnp.where(owner == origins[d], new, cell)
+                outer.append(cell)
+            east = jnp.concatenate([here_j[1:], beside[0][j : j + 1]], axis=0)
+            west = jnp.concatenate([beside[1][j : j + 1], here_j[:-1]], axis=0)
+            above = jnp.where(me_n == nests - 1, here_j[:, rows - 1 :], outer[1])
+            below = jnp.where(me_n == 0, here_j[:, :1], outer[0])
+            north = jnp.where(row_lane == rows - 1, above, pltpu.roll(here_j, rows - 1, 1))
+            south = jnp.where(row_lane == 0, below, pltpu.roll(here_j, 1, 1))
+            result[f] = here_j + rate_ref[f] * (east + west + north + south - 4.0 * here_j)
 
     first()
     lax.fori_loop(1, groups, restrict, 0)
-    stages = {"F": forward, "P": relay, "M": merge, "E": finish}
+    swap_edges()
+    stages = {"F": forward, "P": relay, "M": merge}
     for step in order(groups):
         stages[step[0]](step[1])
 
     for g in range(groups):
         a2a_bytes(g).wait_send()
-    for copy in [*sent.values(), *edges.values()]:
+    for copy in sent.values():
         copy.wait_send()
 
 
@@ -408,10 +459,13 @@
             pltpu.VMEM((groups, 2, LANES // 2, rows), F32),
             pltpu.VMEM((groups, 2, LANES, rows), F32),
             pltpu.VMEM((2, cols, rows), jnp.int32),
-            pltpu.VMEM((groups, 2, per, rows), F32),
-            pltpu.VMEM((groups, 2, per, rows), F32),
-            pltpu.VMEM((groups, 2, cols, LANES), F32),
-            pltpu.VMEM((groups, 2, cols, LANES), F32),
+            pltpu.VMEM((2, planes + 8, rows), F32),
+            pltpu.VMEM((2, planes + 8, rows), F32),
+            pltpu.VMEM((2, cols, LANES), F32),
+            pltpu.VMEM((2, cols, LANES), F32),
+            pltpu.VMEM((groups, 2, nrows // rows, per, rows), F32),
+            pltpu.VMEM((groups, 2, nests, per, rows), F32),
+            pltpu.VMEM((groups, 8 * nests, LANES), F32),
             dma((4,)),
             dma((groups,)),
             dma((CHUNKS,)),
@@ -424,8 +478,12 @@
             dma((groups, 2)),
             dma((groups, 4)),
             dma((groups, 4)),
-            dma((groups, 4)),
-            dma((groups, 4)),
+            dma((4,)),
+            dma((4,)),
+            dma((groups, 2, nests)),
+            dma((groups, 2, nests)),
+            dma((groups, nests - 1)),
+            dma((groups, nests - 1)),
         ],
         compiler_params=pltpu.CompilerParams(
             collective_id=0, has_side_effects=True, vmem_limit_bytes=60 * 2**20

time: 55.4 us -> 58.8 us (1.061)
  Pallas kernels: 54.2 us -> 57.4 us
    pallas_call x1, Pallas kernels: 54.2 us -> 57.4 us  [per_device(): pl.pallas_call(functools.partial(kernel, tiles, nests), out_shape=pltpu.V...]
where the time goes in v3:
time: 58.8 us; the launch traced here: 58.2 us
  Pallas kernels  57.4 us (98%)
  local copies, waits for them, and re-layouts  0.8 us (1%)
    pallas_call x1, Pallas kernels, per_device(): pl.pallas_call(functools.partial(kernel, tiles, nests), out_shape=pltpu.V...  57.4 us

profile of v3, /device:TPU:1, one launch (start us, length us, event | category | flops | bytes accessed | tf_op | source)
XLA Modules:
  0.0 58.2 jit_solution(12202849276598620778)
XLA Ops:
  0.0 57.4 %shard_map.73 = f32[32,16,256]{2,1,0:T(8,128)S(1)} custom-call(s32[2,4]{1,0:T(2,128)} %bitcast.1, f32[32]{0:T(128)} %rate_hbm.1, f32[8,24]{1,0:T(8,128)} %rw_hbm.1, s32[16,256]{1,0:T(8,128)} %prio_hbm.1, f32[1,32,24,3072]{3,2,1,0:T(8,128)} %child_hbm.1, f32[3072,1024]{1,0:T(8,128)} %cw_hbm.1, f32[32,16,256]{2,1,0:T(8,128)} %parent_hbm.1), custom_call_target="tpu_custom_call" | custom-call | tf_op jit(solution)/shard_map/pallas_call | solution.py:438
  57.4 0.8 %copy.9 = f32[32,16,256]{2,1,0:T(8,128)} copy(f32[32,16,256]{2,1,0:T(8,128)S(1)} %shard_map.73) | data formatting | bytes 1048576

commit v4 on v3

--- a/solution.py
+++ b/solution.py
@@ -37,13 +37,11 @@
 
 
 def order(groups):
-    for g in range(groups + 1):
-        if g < groups:
-            yield "F", g
-        if g > 0:
-            yield "M", g - 1
-        if g < groups:
-            yield "P", g
+    for g in range(groups):
+        yield "F", g
+        yield "P", g
+    for g in range(groups):
+        yield "M", g
 
 
 def kernel(

time: 58.8 us -> 53.5 us (0.910)
  Pallas kernels: 57.4 us -> 52.6 us
    pallas_call x1, Pallas kernels: 57.4 us -> 52.6 us  [per_device(): pl.pallas_call(functools.partial(kernel, tiles, nests), out_shape=pltpu.V...]
where the time goes in v4:
time: 53.5 us; the launch traced here: 53.4 us
  Pallas kernels  52.6 us (98%)
  local copies, waits for them, and re-layouts  0.8 us (1%)
    pallas_call x1, Pallas kernels, per_device(): pl.pallas_call(functools.partial(kernel, tiles, nests), out_shape=pltpu.V...  52.6 us

profile of v4, /device:TPU:1, one launch (start us, length us, event | category | flops | bytes accessed | tf_op | source)
XLA Modules:
  0.0 53.4 jit_solution(4708117147398359083)
XLA Ops:
  0.0 52.6 %shard_map.73 = f32[32,16,256]{2,1,0:T(8,128)S(1)} custom-call(s32[2,4]{1,0:T(2,128)} %bitcast.1, f32[32]{0:T(128)} %rate_hbm.1, f32[8,24]{1,0:T(8,128)} %rw_hbm.1, s32[16,256]{1,0:T(8,128)} %prio_hbm.1, f32[1,32,24,3072]{3,2,1,0:T(8,128)} %child_hbm.1, f32[3072,1024]{1,0:T(8,128)} %cw_hbm.1, f32[32,16,256]{2,1,0:T(8,128)} %parent_hbm.1), custom_call_target="tpu_custom_call" | custom-call | tf_op jit(solution)/shard_map/pallas_call | solution.py:436
  52.6 0.8 %copy.9 = f32[32,16,256]{2,1,0:T(8,128)} copy(f32[32,16,256]{2,1,0:T(8,128)S(1)} %shard_map.73) | data formatting | bytes 1048576

commit v5 on v4

--- a/solution.py
+++ b/solution.py
@@ -353,23 +353,6 @@
         if g == 0:
             for side in range(4):
                 sent["old", side].wait_recv()
-        now = merged[g * per : (g + 1) * per]
-        mine = blocks[g, 1 - near].reshape(per, cols, rows)
-        now = jnp.where((prio == me_n)[None], mine, now)
-        for q in range(4):
-            sent["slab", g, q].wait_recv()
-        far_n = lax.rem(me_n + 2, nests)
-        ways = [(prio == n)[None] for n in (low_n, high_n)]
-        far = (prio == far_n)[None]
-        mixed = []
-        for side in range(2):
-            part = now[side * (per // 2) : (side + 1) * (per // 2)]
-            for way in range(2):
-                take = (ways[way] | far) if way == side else ways[way]
-                slab = slabs[g, way, side * half : (side + 1) * half]
-                part = jnp.where(take, slab.reshape(per // 2, cols, rows), part)
-            mixed.append(part)
-        now = jnp.concatenate(mixed, axis=0)
         origins = [lax.rem(me_n + nests - d, nests).astype(F32) for d in range(nests)]
         beside = []
         for side in range(2):
@@ -388,9 +371,9 @@
         ]
         lines.append(jnp.zeros((LANES - 2 * nests, LANES), F32))
         ends = jnp.concatenate(lines, axis=0).T
+        outers = []
         for j in range(per):
             f = g * per + j
-            here_j = now[j]
             outer = []
             for way in range(2):
                 old = ns_old[1 - way]
@@ -400,6 +383,27 @@
                     new = ends[j * cols : (j + 1) * cols, at : at + 1]
                     cell = jnp.where(owner == origins[d], new, cell)
                 outer.append(cell)
+            outers.append(outer)
+        now = merged[g * per : (g + 1) * per]
+        mine = blocks[g, 1 - near].reshape(per, cols, rows)
+        now = jnp.where((prio == me_n)[None], mine, now)
+        for q in range(4):
+            sent["slab", g, q].wait_recv()
+        far_n = lax.rem(me_n + 2, nests)
+        ways = [(prio == n)[None] for n in (low_n, high_n)]
+        far = (prio == far_n)[None]
+        mixed = []
+        for side in range(2):
+            part = now[side * (per // 2) : (side + 1) * (per // 2)]
+            for way in range(2):
+                take = (ways[way] | far) if way == side else ways[way]
+                slab = slabs[g, way, side * half : (side + 1) * half]
+                part = jnp.where(take, slab.reshape(per // 2, cols, rows), part)
+            mixed.append(part)
+        now = jnp.concatenate(mixed, axis=0)
+        for j in range(per):
+            f = g * per + j
+            here_j, outer = now[j], outers[j]
             east = jnp.concatenate([here_j[1:], beside[0][j : j + 1]], axis=0)
             west = jnp.concatenate([beside[1][j : j + 1], here_j[:-1]], axis=0)
             above = jnp.where(me_n == nests - 1, here_j[:, rows - 1 :], outer[1])

time: 53.5 us -> 53.1 us (level)
  no operation moved by 1% of the time
where the time goes in v5:
time: 53.1 us; the launch traced here: 53 us
  Pallas kernels  52.2 us (98%)
  local copies, waits for them, and re-layouts  0.8 us (2%)
    pallas_call x1, Pallas kernels, per_device(): pl.pallas_call(functools.partial(kernel, tiles, nests), out_shape=pltpu.V...  52.2 us

profile of v5, /device:TPU:1, one launch (start us, length us, event | category | flops | bytes accessed | tf_op | source)
XLA Modules:
  0.0 53.0 jit_solution(14811825640958898631)
XLA Ops:
  0.0 52.2 %shard_map.73 = f32[32,16,256]{2,1,0:T(8,128)S(1)} custom-call(s32[2,4]{1,0:T(2,128)} %bitcast.1, f32[32]{0:T(128)} %rate_hbm.1, f32[8,24]{1,0:T(8,128)} %rw_hbm.1, s32[16,256]{1,0:T(8,128)} %prio_hbm.1, f32[1,32,24,3072]{3,2,1,0:T(8,128)} %child_hbm.1, f32[3072,1024]{1,0:T(8,128)} %cw_hbm.1, f32[32,16,256]{2,1,0:T(8,128)} %parent_hbm.1), custom_call_target="tpu_custom_call" | custom-call | tf_op jit(solution)/shard_map/pallas_call | solution.py:440
  52.2 0.8 %copy.9 = f32[32,16,256]{2,1,0:T(8,128)} copy(f32[32,16,256]{2,1,0:T(8,128)S(1)} %shard_map.73) | data formatting | bytes 1048576
